TPU v7x, 256 devices: a whole 4x4x8 slice. The times are simulated.
256 devices in a mesh: dp: 8 (over x, y_lo), expert: 16 (over z, core), tensor: 2 (over y_hi).
Axes of the slice: x: 4, y: 4 (y_hi: 2, y_lo: 2; y = y_hi * 2 + y_lo), z: 8, core: 2. Of those that a mesh axis runs over, the one named last changes fastest.
Arguments:
- tokens: bfloat16 [1536, 256, 1280], P(('dp', 'expert', 'tensor')), may hold values from -16 to 16
- cotangent: bfloat16 [1536, 256, 1280], P(('dp', 'expert', 'tensor')), may hold values from -6 to 6
- norm_gain: float32 [1280], replicated, may hold values from 0.5 to 1.5
- slot_keys: bfloat16 [1280, 32], replicated, may hold values from -2 to 2
- w_in: bfloat16 [16, 1280, 2560], P('expert', None, 'tensor'), may hold values from -0.15625 to 0.15625
- w_out: bfloat16 [16, 2560, 1280], P('expert', 'tensor'), may hold values from -0.125 to 0.125
Outputs:
- grad_tokens: bfloat16 [1536, 256, 1280], P(('dp', 'expert', 'tensor'))
- grad_gain: float32 [1280], replicated
- grad_keys: float32 [1280, 32], replicated
- grad_in: bfloat16 [16, 1280, 2560], P('expert', 'dp', 'tensor')
- grad_out: bfloat16 [16, 2560, 1280], P('expert', 'tensor', 'dp')
All inputs are finite; a program needn't handle non-finite values.
Results may differ from a plain program's by a relative error of at most 0.014.
The roundings to bfloat16 on the way count: a program that leaves them out, or rounds other values in their place, can miss the bound.
Values may be sent and summed in bfloat16 or wider, within the bound.
No kernel may reach another device: no remote copies, remote signals or barrier semaphores. Data moves between devices by JAX's collectives and lax.ppermute only.
A program may use at most 128 MiB of HBM per device.

v0:
```python
import jax
import jax.numpy as jnp
from jax import lax
from jax.sharding import PartitionSpec as P

SLOT_PER = 2
EPSILON = 1e-06


def from_everyone(shard, axis):
    devices = lax.axis_size(axis)
    return lax.all_to_all(
        jnp.broadcast_to(shard[None], (devices, *shard.shape)), axis, 0, 0, tiled=True
    )


def in_order(tiles, dim):
    shape = list(tiles.shape[1:])
    shape[dim] *= tiles.shape[0]
    return jnp.moveaxis(tiles, 0, dim).reshape(shape)


def collect(shard, axis, dim):
    tiles = from_everyone(shard, axis)
    return in_order(tiles, dim)


def in_blocks(shard, dim, devices):
    before, after = (shard.shape[:dim], shard.shape[dim + 1 :])
    return jnp.moveaxis(shard.reshape(*before, devices, -1, *after), dim, 0)


def summed_on_arrival(shard, axis, dim):
    tiles = in_blocks(shard, dim, lax.axis_size(axis))
    arrived = lax.all_to_all(tiles, axis, split_axis=0, concat_axis=0, tiled=True)
    return arrived.sum(axis=0)


def sent_and_summed(shard, axis, dim):
    devices = lax.axis_size(axis)
    tiles = lax.all_to_all(in_blocks(shard, dim, devices), axis, 0, 0, tiled=True)
    return jnp.sum(tiles.astype(jnp.float32), axis=0)


def mixing_forward(tokens, gain, slot_keys):
    average = jnp.mean(tokens, axis=-1, keepdims=True, dtype=jnp.float32)
    centred = tokens.astype(jnp.float32) - average
    spread = jnp.mean(centred * centred, axis=-1, keepdims=True)
    inverse = lax.rsqrt(spread + EPSILON)
    scaled = centred * inverse
    normed = (scaled * gain).astype(jnp.bfloat16)
    logits = jnp.einsum("bmd,dn->bmn", normed, slot_keys, preferred_element_type=jnp.float32)
    dispatch = jax.nn.softmax(logits, axis=1)
    combine = jax.nn.softmax(logits, axis=2)
    dispatch_low = dispatch.astype(jnp.bfloat16)
    slot_values = jnp.einsum(
        "bmn,bmd->bnd", dispatch_low, normed, preferred_element_type=jnp.float32
    )
    return (slot_values, combine, (scaled, inverse, normed, dispatch, combine, dispatch_low))


def mixing_backward(saved, gain, slot_keys, slot_grad, combine_grad):
    scaled, inverse, normed, dispatch, combine, dispatch_low = saved
    grad_dispatch = jnp.einsum(
        "bnd,bmd->bmn", slot_grad, normed, preferred_element_type=jnp.float32
    )
    grad_normed = jnp.einsum(
        "bmn,bnd->bmd", dispatch_low, slot_grad, preferred_element_type=jnp.float32
    )
    grad_logits = dispatch * (
        grad_dispatch - jnp.sum(dispatch * grad_dispatch, axis=1, keepdims=True)
    )
    grad_logits = grad_logits + combine * (
        combine_grad - jnp.sum(combine * combine_grad, axis=2, keepdims=True)
    )
    keys_wide = slot_keys.astype(jnp.float32)
    grad_normed = grad_normed + jnp.einsum(
        "bmn,dn->bmd", grad_logits, keys_wide, precision=lax.Precision.HIGHEST
    )
    keys_term = jnp.einsum(
        "bmd,bmn->dn", normed.astype(jnp.float32), grad_logits, precision=lax.Precision.HIGHEST
    )
    gain_term = jnp.sum(grad_normed * scaled, axis=(0, 1))
    grad_scaled = grad_normed * gain
    first_mean = jnp.mean(grad_scaled, axis=-1, keepdims=True)
    second_mean = jnp.mean(grad_scaled * scaled, axis=-1, keepdims=True)
    grad_tok = inverse * (grad_scaled - first_mean - scaled * second_mean)
    return (grad_tok, gain_term, keys_term)


def contract_rows(left, right):
    return lax.dot_general(
        left, right, (((0,), (0,)), ((), ())), preferred_element_type=jnp.float32
    )


def contract_cols(left, right):
    return lax.dot_general(
        left, right, (((1,), (1,)), ((), ())), preferred_element_type=jnp.float32
    )


def local(tokens, cotangent, norm_gain, slot_keys, w_in, w_out):
    local_imgs, token_count, features = tokens.shape
    slot_count = slot_keys.shape[1]
    experts = slot_count // SLOT_PER
    slot_values, combine, saved = mixing_forward(tokens, norm_gain, slot_keys)
    slot_inputs = slot_values.astype(jnp.bfloat16).reshape(local_imgs, experts, SLOT_PER, features)
    arrived = lax.all_to_all(slot_inputs, "expert", split_axis=1, concat_axis=0, tiled=True)
    slot_rows = collect(arrived, "tensor", 0).reshape(-1, features)
    first_proj = w_in[0]
    second_proj = w_out[0]
    pre_act = jnp.dot(slot_rows, first_proj, preferred_element_type=jnp.float32)
    hidden = jax.nn.gelu(pre_act).astype(jnp.bfloat16)
    segment = hidden
    outputs = summed_on_arrival(
        jnp.dot(segment, second_proj, preferred_element_type=jnp.float32), "tensor", 0
    )
    outputs = outputs.astype(jnp.bfloat16).reshape(arrived.shape)
    returned = lax.all_to_all(outputs, "expert", split_axis=0, concat_axis=1, tiled=True).reshape(
        local_imgs, slot_count, features
    )
    combine_low = combine.astype(jnp.bfloat16)
    grad_slots = jnp.einsum(
        "bmn,bmd->bnd", combine_low, cotangent, preferred_element_type=jnp.float32
    )
    grad_slots = grad_slots.astype(jnp.bfloat16).reshape(local_imgs, experts, SLOT_PER, features)
    grad_combine = jnp.einsum(
        "bmd,bnd->bmn", cotangent, returned, preferred_element_type=jnp.float32
    )
    grads_sent = lax.all_to_all(grad_slots, "expert", split_axis=1, concat_axis=0, tiled=True)
    grad_rows = collect(grads_sent, "tensor", 0).reshape(-1, features)
    grad_hidden = contract_cols(grad_rows, second_proj)
    grad_pre = jax.vjp(jax.nn.gelu, pre_act)[1](grad_hidden)[0].astype(jnp.bfloat16)
    segment = grad_pre
    grad_in_rows = sent_and_summed(
        contract_cols(segment, first_proj).astype(jnp.bfloat16), "tensor", 0
    )
    grad_in_rows = grad_in_rows.astype(jnp.bfloat16).reshape(arrived.shape)
    grad_back = lax.all_to_all(
        grad_in_rows, "expert", split_axis=0, concat_axis=1, tiled=True
    ).reshape(local_imgs, slot_count, features)
    grad_tok, gain_term, keys_term = mixing_backward(
        saved, norm_gain, slot_keys, grad_back, grad_combine
    )
    grad_tokens = (cotangent.astype(jnp.float32) + grad_tok).astype(jnp.bfloat16)
    grad_gain, grad_keys = lax.psum((gain_term, keys_term), ("dp", "expert", "tensor"))
    columns = slot_rows
    grad_first = lax.psum_scatter(
        contract_rows(columns, grad_pre).astype(jnp.bfloat16), "dp", scatter_dimension=0, tiled=True
    )
    columns = grad_rows
    grad_second = (
        lax.psum_scatter(
            contract_rows(columns, hidden).astype(jnp.bfloat16),
            "dp",
            scatter_dimension=0,
            tiled=True,
        )
        .astype(jnp.float32)
        .T
    )
    return (
        grad_tokens,
        grad_gain,
        grad_keys,
        grad_first[None],
        grad_second.astype(jnp.bfloat16)[None],
    )


def solution(mesh):
    placed = (
        P(("dp", "expert", "tensor"), None, None),
        P(("dp", "expert", "tensor"), None, None),
        P(),
        P(),
        P("expert", None, "tensor"),
        P("expert", "tensor", None),
    )
    return jax.shard_map(
        local,
        mesh=mesh,
        in_specs=placed,
        out_specs=(
            P(("dp", "expert", "tensor"), None, None),
            P(),
            P(),
            P("expert", "dp", "tensor"),
            P("expert", "tensor", "dp"),
        ),
        check_vma=False,
    )
```

profile of v0, /device:TPU:1, one launch (start us, length us, event | category | flops | bytes accessed | tf_op | source)
XLA Modules:
  0.0 502.3 jit_solution(15583305845671244630)
XLA Ops:
  8.0 2.8 convert_reduce_fusion
  10.9 0.6 copy-done.2
  11.5 1.2 fusion.15
  12.7 1.7 fusion.42
  14.4 0.7 copy-done.4
  15.5 3.8 convolution_convert_fusion.3
  19.3 2.0 reshape.79
  21.3 2.1 copy.15
  23.5 10.0 %all-to-all-start = ((bf16[6,16,2,1280]{3,2,0,1:T(2,128)(2,1)}), bf16[6,16,2,1280]{3,2,0,1:T(2,128)(2,1)}, u32[]{:S(2)}, u32[]{:S(2)}) async-start(bf16[6,16,2,1280]{3,2,0,1:T(2,128)(2,1)} %copy.15), calls=%async_computation | async-start | bytes 983040 | tf_op jit(solution)/shard_map/all_to_all | solution.py:131
  33.4 1.8 fusion.52
  35.2 4.6 convolution_convert_fusion.2
  39.8 2.0 reshape.80
  41.9 2.1 copy.16
  44.0 6.1 %all-to-all-done = bf16[6,16,2,1280]{3,2,0,1:T(2,128)(2,1)} async-done(((bf16[6,16,2,1280]{3,2,0,1:T(2,128)(2,1)}), bf16[6,16,2,1280]{3,2,0,1:T(2,128)(2,1)}, u32[]{:S(2)}, u32[]{:S(2)}) %all-to-all-start) | async-done | bytes 491552 | tf_op jit(solution)/shard_map/all_to_all | solution.py:131
  50.1 19.4 %all_to_all.80 = bf16[6,16,2,1280]{3,2,0,1:T(2,128)(2,1)S(1)} all-to-all(bf16[6,16,2,1280]{3,2,0,1:T(2,128)(2,1)} %copy.16), channel_id=1, replica_groups=mesh['dp'=8,'expert'=16,'tensor'=2] {'expert'}, dimensions={1} | all-to-all | bytes 983040 | tf_op jit(solution)/shard_map/all_to_all | solution.py:109
  69.5 0.5 broadcast_in_dim.15
  70.0 18.9 %all_to_all.81 = bf16[2,96,1,2,1280]{4,3,2,1,0:T(2,128)(2,1)} all-to-all(bf16[2,96,1,2,1280]{4,3,2,1,0:T(2,128)(2,1)S(1)} %broadcast_in_dim.15), channel_id=1, replica_groups=mesh['dp'=8,'expert'=16,'tensor'=2] {'tensor'}, dimensions={0} | all-to-all | bytes 1966080 | tf_op jit(solution)/shard_map/all_to_all | solution.py:12
  88.9 2.5 broadcast_in_dim.13
  91.4 4.6 all-to-all-start.1
  96.0 3.3 reshape_reshape.7
  99.3 4.4 multiply_convert_fusion
  103.7 6.3 %all-to-all-done.1 = bf16[2,96,1,2,1280]{4,3,2,1,0:T(2,128)(2,1)} async-done(((bf16[2,96,1,2,1280]{4,3,2,1,0:T(2,128)(2,1)}), bf16[2,96,1,2,1280]{4,3,2,1,0:T(2,128)(2,1)}, u32[]{:S(2)}, u32[]{:S(2)}) %all-to-all-start.1) | async-done | bytes 983072 | tf_op jit(solution)/shard_map/all_to_all | solution.py:12
  110.0 3.3 reshape_reshape.6
  113.3 4.9 fusion.33
  118.2 2.4 fusion.24
  120.7 3.6 all-to-all-start.4
  124.2 4.9 fusion.16
  129.2 8.3 %all-to-all-done.4 = bf16[2,192,1280]{2,1,0:T(8,128)(2,1)S(1)} async-done(((bf16[2,192,1280]{2,1,0:T(8,128)(2,1)}), bf16[2,192,1280]{2,1,0:T(8,128)(2,1)S(1)}, u32[]{:S(2)}, u32[]{:S(2)}) %all-to-all-start.4) | async-done | bytes 983072 | tf_op jit(solution)/shard_map/all_to_all | solution.py:41
  137.5 3.7 all-to-all-start.6
  141.2 1.1 reduce_sum.106
  142.3 2.0 reshape.82
  144.3 19.8 %all-to-all-done.6 = f32[2,192,1280]{2,1,0:T(8,128)S(1)} async-done(((f32[2,192,1280]{2,1,0:T(8,128)}), f32[2,192,1280]{2,1,0:T(8,128)S(1)}, u32[]{:S(2)}, u32[]{:S(2)}) %all-to-all-start.6) | async-done | bytes 1966112 | tf_op jit(solution)/shard_map/all_to_all | solution.py:35
  164.1 6.3 %all-to-all-start.5 = ((bf16[96,1,2,1280]{3,2,1,0:T(2,128)(2,1)}), bf16[96,1,2,1280]{3,2,1,0:T(2,128)(2,1)S(1)}, u32[]{:S(2)}, u32[]{:S(2)}) async-start(bf16[96,1,2,1280]{3,2,1,0:T(2,128)(2,1)} %reshape.82), calls=%async_computation.5 | async-start | bytes 983040 | tf_op jit(solution)/shard_map/all_to_all | solution.py:140
  170.5 1.0 convert_element_type.73
  171.5 15.6 %all-to-all-done.5 = bf16[96,1,2,1280]{3,2,1,0:T(2,128)(2,1)S(1)} async-done(((bf16[96,1,2,1280]{3,2,1,0:T(2,128)(2,1)}), bf16[96,1,2,1280]{3,2,1,0:T(2,128)(2,1)S(1)}, u32[]{:S(2)}, u32[]{:S(2)}) %all-to-all-start.5) | async-done | bytes 491552 | tf_op jit(solution)/shard_map/all_to_all | solution.py:140
  187.1 3.5 all-to-all-start.7
  191.4 3.5 multiply_reduce_fusion.2
  194.8 11.7 %all-to-all-done.7 = bf16[96,1,2,1280]{3,2,1,0:T(2,128)(2,1)S(1)} async-done(((bf16[96,1,2,1280]{3,2,1,0:T(2,128)(2,1)}), bf16[96,1,2,1280]{3,2,1,0:T(2,128)(2,1)S(1)}, u32[]{:S(2)}, u32[]{:S(2)}) %all-to-all-start.7) | async-done | bytes 491552 | tf_op jit(solution)/shard_map/all_to_all | solution.py:120
  207.0 3.5 multiply_reduce_fusion.1
  210.7 2.9 convolution_bitcast_fusion
  213.7 5.0 convolution_convert_fusion.1
  219.0 4.9 convolution_convert_fusion
  224.0 5.6 %fusion.44 = f32[6,256,1280]{2,1,0:T(8,128)} fusion(bf16[6,32,1280]{2,1,0:T(8,128)(2,1)S(1)} %reshape.83, f32[6,32]{1,0:T(8,128)S(1)} %get-tuple-element.8, f32[6,256,32]{1,2,0:T(8,128)} %copy-done.4), kind=kOutput, calls=%fused_computation.58 | convolution fusion | flops 125977024 | bytes 8553216 | tf_op jit(solution)/shard_map/bmn,bnd->bmd/dot_general | solution.py:67
  229.6 10.7 %fusion.14 = (f32[1280]{0:T(1024)S(1)}, f32[6,256]{1,0:T(8,128)S(1)}, f32[6,256]{1,0:T(8,128)S(1)}, f32[6,256,1280]{2,1,0:T(8,128)}) fusion(bf16[6,256,1280]{2,1,0:T(8,128)(2,1)} %param.6, f32[6,256]{1,0:T(8,128)S(1)} %add_rsqrt_fusion, f32[6,256]{1,0:T(8,128)S(1)} %broadcast_multiply_fusion.2, f32[1280]{0:T(1024)S(1)} %copy-done.10, ...), kind=kOutput, calls=%fused_computation.16 | convolution fusion | flops 774631168 | bytes 19974144 | tf_op jit(solution)/shard_map/bmn,dn->bmd/dot_general | solution.py:77
  240.2 79.7 %psum.14 = f32[1280]{0:T(1024)} all-reduce(f32[1280]{0:T(1024)S(1)} %get-tuple-element.5), channel_id=1, replica_groups=mesh['dp'=8,'expert'=16,'tensor'=2] {'dp','expert','tensor'}, use_global_device_ids=true, to_apply=%region_13.0 | all-reduce | flops 1280 | bytes 10240 | tf_op jit(solution)/shard_map/psum | solution.py:147
  319.9 8.7 %fusion.13 = bf16[6,256,1280]{2,1,0:T(8,128)(2,1)} fusion(bf16[6,256,1280]{2,1,0:T(8,128)(2,1)} %param.6, bf16[6,256,1280]{2,1,0:T(8,128)(2,1)} %param.7, f32[6,256,1280]{2,1,0:T(8,128)} %get-tuple-element.18, f32[6,256]{1,0:T(8,128)S(1)} %get-tuple-element.19, f32[6,256]{1,0:T(8,128)S(1)} %get-tuple-element.20, f32[1280]{0:T(1024)S(1)} %copy-done.10, ...), kind=kLoop, calls=%fused_computation.15 | loop fusion | flops 21626880 | bytes 19690496 | tf_op jit(solution)/shard_map/convert_element_type | solution.py:146
  328.6 164.7 %all-reduce.2.cloned.1.call-done = f32[1280,32]{0,1:T(8,128)} async-done(((f32[1280,32]{0,1:T(8,128)}), f32[1280,32]{0,1:T(8,128)}) %all-reduce.2.cloned.1.call-update) | async-done | bytes 163856 | tf_op jit(solution)/shard_map/psum | solution.py:147
  493.3 1.6 copy.20
  (40 shorter events, 2.4 us)
Async XLA Ops:
  8.0 91.3 %copy-start = (bf16[1,1280,1280]{2,1,0:T(8,128)(2,1)S(1)}, bf16[1,1280,1280]{2,1,0:T(8,128)(2,1)}, u32[]{:S(2)}) copy-start(bf16[1,1280,1280]{2,1,0:T(8,128)(2,1)} %param.10) | copy-start | bytes 9830404
  8.0 3.4 copy-start.2
  8.0 4.6 copy-start.10
  8.0 4.6 copy-start.8
  14.4 0.7 copy-start.4
  23.5 26.6 %all-to-all-start = ((bf16[6,16,2,1280]{3,2,0,1:T(2,128)(2,1)}), bf16[6,16,2,1280]{3,2,0,1:T(2,128)(2,1)}, u32[]{:S(2)}, u32[]{:S(2)}) async-start(bf16[6,16,2,1280]{3,2,0,1:T(2,128)(2,1)} %copy.15), calls=%async_computation | async-start | bytes 983040 | tf_op jit(solution)/shard_map/all_to_all | solution.py:131
  91.4 18.6 %all-to-all-start.1 = ((bf16[2,96,1,2,1280]{4,3,2,1,0:T(2,128)(2,1)}), bf16[2,96,1,2,1280]{4,3,2,1,0:T(2,128)(2,1)}, u32[]{:S(2)}, u32[]{:S(2)}) async-start(bf16[2,96,1,2,1280]{4,3,2,1,0:T(2,128)(2,1)} %broadcast_in_dim.13), calls=%async_computation.1 | async-start | bytes 1966080 | tf_op jit(solution)/shard_map/all_to_all | solution.py:12
  118.2 2.4 copy-start.11
  120.7 16.8 %all-to-all-start.4 = ((bf16[2,192,1280]{2,1,0:T(8,128)(2,1)}), bf16[2,192,1280]{2,1,0:T(8,128)(2,1)S(1)}, u32[]{:S(2)}, u32[]{:S(2)}) async-start(bf16[2,192,1280]{2,1,0:T(8,128)(2,1)} %bitcast.77), calls=%async_computation.4 | async-start | bytes 1966080 | tf_op jit(solution)/shard_map/all_to_all | solution.py:41
  137.5 26.6 %all-to-all-start.6 = ((f32[2,192,1280]{2,1,0:T(8,128)}), f32[2,192,1280]{2,1,0:T(8,128)S(1)}, u32[]{:S(2)}, u32[]{:S(2)}) async-start(f32[2,192,1280]{2,1,0:T(8,128)} %fusion.16), calls=%async_computation.6 | async-start | bytes 3932160 | tf_op jit(solution)/shard_map/all_to_all | solution.py:35
  144.3 47.1 %copy-start.7 = (f32[6,256,32]{1,2,0:T(8,128)S(1)}, f32[6,256,32]{1,2,0:T(8,128)}, u32[]{:S(2)}) copy-start(f32[6,256,32]{1,2,0:T(8,128)} %get-tuple-element.9) | copy-start | bytes 589828
  164.1 23.0 %all-to-all-start.5 = ((bf16[96,1,2,1280]{3,2,1,0:T(2,128)(2,1)}), bf16[96,1,2,1280]{3,2,1,0:T(2,128)(2,1)S(1)}, u32[]{:S(2)}, u32[]{:S(2)}) async-start(bf16[96,1,2,1280]{3,2,1,0:T(2,128)(2,1)} %reshape.82), calls=%async_computation.5 | async-start | bytes 983040 | tf_op jit(solution)/shard_map/all_to_all | solution.py:140
  187.1 19.4 %all-to-all-start.7 = ((bf16[96,1,2,1280]{3,2,1,0:T(2,128)(2,1)}), bf16[96,1,2,1280]{3,2,1,0:T(2,128)(2,1)S(1)}, u32[]{:S(2)}, u32[]{:S(2)}) async-start(bf16[96,1,2,1280]{3,2,1,0:T(2,128)(2,1)} %convert_element_type.73), calls=%async_computation.7 | async-start | bytes 983040 | tf_op jit(solution)/shard_map/all_to_all | solution.py:120
  190.5 302.7 %all-reduce.2.cloned.1.call-start = ((), (), s32[]{:S(2)}) async-start(), calls=%async_computation.10 | async-start | bytes 327680 | tf_op jit(solution)/shard_map/psum | solution.py:147
  207.0 3.7 copy-start.3
  210.7 3.0 copy-start.6
  213.6 5.4 %copy-start.5 = (bf16[384,1280]{1,0:T(8,128)(2,1)S(1)}, bf16[384,1280]{1,0:T(8,128)(2,1)}, u32[]{:S(2)}) copy-start(bf16[384,1280]{1,0:T(8,128)(2,1)} %reshape_reshape.6) | copy-start | bytes 2949124
  213.7 279.6 %reduce-scatter.3.cloned.1.call-start = ((), (), s32[]{:S(2)}) async-start(), calls=%async_computation.11 | async-start | bytes 3686400 | tf_op jit(solution)/shard_map/reduce_scatter | solution.py:149
  218.7 274.5 %reduce-scatter.5.cloned.1.call-start = ((), (), s32[]{:S(2)}) async-start(), calls=%async_computation.12 | async-start | bytes 3686400 | tf_op jit(solution)/shard_map/reduce_scatter | solution.py:154
  224.0 5.6 %copy-start.9 = (bf16[1280,32]{0,1:T(8,128)(2,1)S(1)}, bf16[1280,32]{0,1:T(8,128)(2,1)}, u32[]{:S(2)}) copy-start(bf16[1280,32]{0,1:T(8,128)(2,1)} %param.9) | copy-start | bytes 245764
  319.9 174.9 %copy-start.1 = (bf16[1,1280,1280]{2,1,0:T(8,128)(2,1)S(1)}, bf16[1,1280,1280]{2,1,0:T(8,128)(2,1)}, u32[]{:S(2)}) copy-start(bf16[1,1280,1280]{2,1,0:T(8,128)(2,1)} %param.10) | copy-start | bytes 9830404
Sparse Core Ops, SparseCore 0:
  213.8 279.4 all-reduce.1
Sparse Core Ops, SparseCore 1:
  218.8 71.0 reduce-scatter.2
  292.9 76.7 reduce-scatter.4
where the time goes:
time: 504 us; the launch traced here: 502 us
  waiting for transfers between devices  232 us (46%)
  blocking collectives  118 us (23%)
  matrix products  62.9 us (12%)
  starting transfers between devices  32.3 us (6%)
  local copies, waits for them, and re-layouts  24.8 us (5%)
  other arithmetic  16.2 us (3%)
  between operations  15.7 us (3%)
    psum x1, waiting for transfers between devices, local(): lax.psum((gain_term, keys_term), ('dp', 'expert', 'tensor'))  165 us
    psum x1, blocking collectives, local(): lax.psum((gain_term, keys_term), ('dp', 'expert', 'tensor'))  79.7 us
    all_to_all x1, waiting for transfers between devices, summed_on_arrival(): lax.all_to_all(tiles, axis, split_axis=0, concat_axis=0, tiled=True)  19.8 us
    all_to_all x1, blocking collectives, local(): lax.all_to_all(slot_inputs, 'expert', split_axis=1, concat_axis=0, tiled=...  19.4 us
    all_to_all x1, blocking collectives, from_everyone(): lax.all_to_all(jnp.broadcast_to(shard[None], (devices, *shard.shape)), ax...  18.9 us
    all_to_all x1, waiting for transfers between devices, local(): lax.all_to_all(grad_in_rows, 'expert', split_axis=0, concat_axis=1, tiled...  15.6 us
    all_to_all x1, waiting for transfers between devices, local(): lax.all_to_all(outputs, 'expert', split_axis=0, concat_axis=1, tiled=True)  11.7 us
    dot_general x1, matrix products, mixing_backward(): jnp.einsum('bmn,dn->bmd', grad_logits, keys_wide, precision=lax.Precision...  10.7 us
  transfers between devices with their start and end apart: 9, of which 7 were waited for; matrix products, arithmetic and copies ran while one was open for 13% of the time, Pallas kernels for 0%

commit v1 on v0

--- a/solution.py
+++ b/solution.py
@@ -144,7 +144,7 @@
         saved, norm_gain, slot_keys, grad_back, grad_combine
     )
     grad_tokens = (cotangent.astype(jnp.float32) + grad_tok).astype(jnp.bfloat16)
-    grad_gain, grad_keys = lax.psum((gain_term, keys_term), ("dp", "expert", "tensor"))
+    grad_gain, grad_keys = lax.psum(lax.psum((gain_term, keys_term), ("expert", "tensor")), "dp")
     columns = slot_rows
     grad_first = lax.psum_scatter(
         contract_rows(columns, grad_pre).astype(jnp.bfloat16), "dp", scatter_dimension=0, tiled=True

time: 504 us -> 718 us (1.42)
  waiting for transfers between devices: 232 us -> 444 us
    psum x1 -> x2, waiting for transfers between devices: 165 us -> 260 us  [the longest x1 260 us: local(): lax.psum((gain_term, keys_term), ('expert', 'tensor'))]
    reduce_scatter x1, waiting for transfers between devices: 0.01 us -> 78.9 us  [local(): lax.psum_scatter(contract_rows(columns, hidden).astype(jnp.bfloat16), 'dp...]
    reduce_scatter x1, waiting for transfers between devices: 0.01 us -> 37.7 us  [local(): lax.psum_scatter(contract_rows(columns, grad_pre).astype(jnp.bfloat16), '...]
    psum x1 -> x2, blocking collectives: 79.7 us -> 83.5 us  [the longest x1 65 us: local(): lax.psum((gain_term, keys_term), ('expert', 'tensor'))]
  transfers between devices with their start and end apart: 9 -> 10, of which waited for: 7 -> 9; matrix products, arithmetic and copies ran while one was open for 13% -> 9% of each run, Pallas kernels for 0% -> 0%
where the time goes in v1:
time: 718 us; the launch traced here: 716 us
  waiting for transfers between devices  444 us (62%)
  blocking collectives  122 us (17%)
  matrix products  62.7 us (9%)
  starting transfers between devices  32.3 us (4%)
  local copies, waits for them, and re-layouts  24.8 us (3%)
  other arithmetic  16.1 us (2%)
  between operations  14 us (2%)
    psum x1, waiting for transfers between devices, local(): lax.psum((gain_term, keys_term), ('expert', 'tensor'))  260 us
    reduce_scatter x1, waiting for transfers between devices, local(): lax.psum_scatter(contract_rows(columns, hidden).astype(jnp.bfloat16), 'dp...  78.9 us
    psum x1, blocking collectives, local(): lax.psum((gain_term, keys_term), ('expert', 'tensor'))  65 us
    reduce_scatter x1, waiting for transfers between devices, local(): lax.psum_scatter(contract_rows(columns, grad_pre).astype(jnp.bfloat16), '...  37.7 us
    all_to_all x1, waiting for transfers between devices, summed_on_arrival(): lax.all_to_all(tiles, axis, split_axis=0, concat_axis=0, tiled=True)  19.8 us
    all_to_all x1, blocking collectives, local(): lax.all_to_all(slot_inputs, 'expert', split_axis=1, concat_axis=0, tiled=...  19.4 us
    all_to_all x1, blocking collectives, from_everyone(): lax.all_to_all(jnp.broadcast_to(shard[None], (devices, *shard.shape)), ax...  18.9 us
    psum x1, blocking collectives, local(): lax.psum(lax.psum((gain_term, keys_term), ('expert', 'tensor')), 'dp')  18.5 us
  transfers between devices with their start and end apart: 10, of which 9 were waited for; matrix products, arithmetic and copies ran while one was open for 9% of the time, Pallas kernels for 0%

profile of v1, /device:TPU:1, one launch (start us, length us, event | category | flops | bytes accessed | tf_op | source)
XLA Modules:
  0.0 716.1 jit_solution(10702119492185686737)
XLA Ops:
  7.2 2.8 convert_reduce_fusion
  10.6 1.2 fusion.15
  11.8 1.7 fusion.42
  14.7 3.8 convolution_convert_fusion.3
  18.5 2.0 reshape.79
  20.5 2.1 copy.15
  22.6 10.0 %all-to-all-start = ((bf16[6,16,2,1280]{3,2,0,1:T(2,128)(2,1)}), bf16[6,16,2,1280]{3,2,0,1:T(2,128)(2,1)}, u32[]{:S(2)}, u32[]{:S(2)}) async-start(bf16[6,16,2,1280]{3,2,0,1:T(2,128)(2,1)} %copy.15), calls=%async_computation | async-start | bytes 983040 | tf_op jit(solution)/shard_map/all_to_all | solution.py:131
  32.6 1.8 fusion.52
  34.4 4.6 convolution_convert_fusion.2
  39.0 2.0 reshape.80
  41.0 2.1 copy.16
  43.2 6.1 all-to-all-done
  49.2 19.4 %all_to_all.80 = bf16[6,16,2,1280]{3,2,0,1:T(2,128)(2,1)S(1)} all-to-all(bf16[6,16,2,1280]{3,2,0,1:T(2,128)(2,1)} %copy.16), channel_id=1, replica_groups=mesh['dp'=8,'expert'=16,'tensor'=2] {'expert'}, dimensions={1} | all-to-all | bytes 983040 | tf_op jit(solution)/shard_map/all_to_all | solution.py:109
  69.2 18.9 %all_to_all.81 = bf16[2,96,1,2,1280]{4,3,2,1,0:T(2,128)(2,1)} all-to-all(bf16[2,96,1,2,1280]{4,3,2,1,0:T(2,128)(2,1)S(1)} %broadcast_in_dim.15), channel_id=1, replica_groups=mesh['dp'=8,'expert'=16,'tensor'=2] {'tensor'}, dimensions={0} | all-to-all | bytes 1966080 | tf_op jit(solution)/shard_map/all_to_all | solution.py:12
  88.1 2.5 broadcast_in_dim.13
  90.6 4.6 all-to-all-start.1
  95.1 3.3 reshape_reshape.7
  98.5 4.4 multiply_convert_fusion
  102.9 6.3 all-to-all-done.1
  109.2 3.3 reshape_reshape.6
  112.5 4.9 fusion.33
  117.4 2.4 fusion.24
  119.8 3.6 all-to-all-start.4
  123.4 4.9 fusion.16
  128.3 8.3 %all-to-all-done.4 = bf16[2,192,1280]{2,1,0:T(8,128)(2,1)S(1)} async-done(((bf16[2,192,1280]{2,1,0:T(8,128)(2,1)}), bf16[2,192,1280]{2,1,0:T(8,128)(2,1)S(1)}, u32[]{:S(2)}, u32[]{:S(2)}) %all-to-all-start.4) | async-done | bytes 983072 | tf_op jit(solution)/shard_map/all_to_all | solution.py:41
  136.6 3.7 all-to-all-start.6
  140.4 1.1 reduce_sum.106
  141.4 2.0 reshape.82
  143.5 19.8 %all-to-all-done.6 = f32[2,192,1280]{2,1,0:T(8,128)S(1)} async-done(((f32[2,192,1280]{2,1,0:T(8,128)}), f32[2,192,1280]{2,1,0:T(8,128)S(1)}, u32[]{:S(2)}, u32[]{:S(2)}) %all-to-all-start.6) | async-done | bytes 1966112 | tf_op jit(solution)/shard_map/all_to_all | solution.py:35
  163.3 6.3 all-to-all-start.5
  169.7 1.0 convert_element_type.73
  170.7 15.6 %all-to-all-done.5 = bf16[96,1,2,1280]{3,2,1,0:T(2,128)(2,1)S(1)} async-done(((bf16[96,1,2,1280]{3,2,1,0:T(2,128)(2,1)}), bf16[96,1,2,1280]{3,2,1,0:T(2,128)(2,1)S(1)}, u32[]{:S(2)}, u32[]{:S(2)}) %all-to-all-start.5) | async-done | bytes 491552 | tf_op jit(solution)/shard_map/all_to_all | solution.py:140
  186.2 3.5 all-to-all-start.7
  190.5 3.5 multiply_reduce_fusion.2
  194.0 11.7 %all-to-all-done.7 = bf16[96,1,2,1280]{3,2,1,0:T(2,128)(2,1)S(1)} async-done(((bf16[96,1,2,1280]{3,2,1,0:T(2,128)(2,1)}), bf16[96,1,2,1280]{3,2,1,0:T(2,128)(2,1)S(1)}, u32[]{:S(2)}, u32[]{:S(2)}) %all-to-all-start.7) | async-done | bytes 491552 | tf_op jit(solution)/shard_map/all_to_all | solution.py:120
  206.2 3.5 multiply_reduce_fusion.1
  209.9 2.9 convolution_bitcast_fusion
  212.9 260.0 %all-reduce.3.cloned.1.call-done = f32[1280,32]{0,1:T(8,128)} async-done(((f32[1280,32]{0,1:T(8,128)}), f32[1280,32]{0,1:T(8,128)}) %all-reduce.3.cloned.1.call-update) | async-done | bytes 163856 | tf_op jit(solution)/shard_map/psum | solution.py:147
  473.0 5.0 convolution_convert_fusion.1
  478.3 4.9 convolution_convert_fusion
  483.2 5.5 fusion.44
  488.7 10.6 %fusion.14 = (f32[1280]{0:T(1024)S(1)}, f32[6,256]{1,0:T(8,128)S(1)}, f32[6,256]{1,0:T(8,128)S(1)}, f32[6,256,1280]{2,1,0:T(8,128)}) fusion(bf16[6,256,1280]{2,1,0:T(8,128)(2,1)} %param.6, f32[6,256]{1,0:T(8,128)S(1)} %add_rsqrt_fusion, f32[6,256]{1,0:T(8,128)S(1)} %broadcast_multiply_fusion.2, f32[1280]{0:T(1024)S(1)} %copy-done.10, ...), kind=kOutput, calls=%fused_computation.16 | convolution fusion | flops 774631168 | bytes 19974144 | tf_op jit(solution)/shard_map/bmn,dn->bmd/dot_general | solution.py:77
  499.3 65.0 %psum.28 = f32[1280]{0:T(1024)S(1)} all-reduce(f32[1280]{0:T(1024)S(1)} %get-tuple-element.5), channel_id=1, replica_groups=mesh['dp'=8,'expert'=16,'tensor'=2] {'expert','tensor'}, use_global_device_ids=true, to_apply=%region_13.0 | all-reduce | flops 1280 | bytes 10240 | tf_op jit(solution)/shard_map/psum | solution.py:147
  564.3 18.5 %psum.29 = f32[1280]{0:T(1024)} all-reduce(f32[1280]{0:T(1024)S(1)} %psum.28), channel_id=1, replica_groups=mesh['dp'=8,'expert'=16,'tensor'=2] {'dp'}, use_global_device_ids=true, to_apply=%region_14.0 | all-reduce | flops 1280 | bytes 10240 | tf_op jit(solution)/shard_map/psum | solution.py:147
  582.8 8.6 %fusion.13 = bf16[6,256,1280]{2,1,0:T(8,128)(2,1)} fusion(bf16[6,256,1280]{2,1,0:T(8,128)(2,1)} %param.6, bf16[6,256,1280]{2,1,0:T(8,128)(2,1)} %param.7, f32[6,256,1280]{2,1,0:T(8,128)} %get-tuple-element.18, f32[6,256]{1,0:T(8,128)S(1)} %get-tuple-element.19, f32[6,256]{1,0:T(8,128)S(1)} %get-tuple-element.20, f32[1280]{0:T(1024)S(1)} %copy-done.10, ...), kind=kLoop, calls=%fused_computation.15 | loop fusion | flops 21626880 | bytes 19690496 | tf_op jit(solution)/shard_map/convert_element_type | solution.py:146
  591.4 37.7 %reduce-scatter.3.cloned.1.call-done = bf16[160,1280]{1,0:T(8,128)(2,1)} async-done(((bf16[1280,1280]{1,0:T(8,128)(2,1)}), bf16[160,1280]{1,0:T(8,128)(2,1)}) %reduce-scatter.3.cloned.1.call-update) | async-done | bytes 409616 | tf_op jit(solution)/shard_map/reduce_scatter | solution.py:149
  629.1 78.9 %reduce-scatter.5.cloned.1.call-done = bf16[160,1280]{1,0:T(8,128)(2,1)} async-done(((bf16[1280,1280]{1,0:T(8,128)(2,1)}), bf16[160,1280]{1,0:T(8,128)(2,1)}) %reduce-scatter.5.cloned.1.call-update) | async-done | bytes 409616 | tf_op jit(solution)/shard_map/reduce_scatter | solution.py:154
  708.0 1.6 copy.21
  (44 shorter events, 4.2 us)
Async XLA Ops:
  7.2 91.3 %copy-start = (bf16[1,1280,1280]{2,1,0:T(8,128)(2,1)S(1)}, bf16[1,1280,1280]{2,1,0:T(8,128)(2,1)}, u32[]{:S(2)}) copy-start(bf16[1,1280,1280]{2,1,0:T(8,128)(2,1)} %param.10) | copy-start | bytes 9830404
  7.2 3.4 copy-start.2
  7.2 4.6 copy-start.10
  7.2 4.6 copy-start.8
  13.6 0.7 copy-start.4
  22.6 26.6 %all-to-all-start = ((bf16[6,16,2,1280]{3,2,0,1:T(2,128)(2,1)}), bf16[6,16,2,1280]{3,2,0,1:T(2,128)(2,1)}, u32[]{:S(2)}, u32[]{:S(2)}) async-start(bf16[6,16,2,1280]{3,2,0,1:T(2,128)(2,1)} %copy.15), calls=%async_computation | async-start | bytes 983040 | tf_op jit(solution)/shard_map/all_to_all | solution.py:131
  90.6 18.6 %all-to-all-start.1 = ((bf16[2,96,1,2,1280]{4,3,2,1,0:T(2,128)(2,1)}), bf16[2,96,1,2,1280]{4,3,2,1,0:T(2,128)(2,1)}, u32[]{:S(2)}, u32[]{:S(2)}) async-start(bf16[2,96,1,2,1280]{4,3,2,1,0:T(2,128)(2,1)} %broadcast_in_dim.13), calls=%async_computation.1 | async-start | bytes 1966080 | tf_op jit(solution)/shard_map/all_to_all | solution.py:12
  117.4 2.4 copy-start.11
  119.8 16.8 %all-to-all-start.4 = ((bf16[2,192,1280]{2,1,0:T(8,128)(2,1)}), bf16[2,192,1280]{2,1,0:T(8,128)(2,1)S(1)}, u32[]{:S(2)}, u32[]{:S(2)}) async-start(bf16[2,192,1280]{2,1,0:T(8,128)(2,1)} %bitcast.77), calls=%async_computation.4 | async-start | bytes 1966080 | tf_op jit(solution)/shard_map/all_to_all | solution.py:41
  136.6 26.7 %all-to-all-start.6 = ((f32[2,192,1280]{2,1,0:T(8,128)}), f32[2,192,1280]{2,1,0:T(8,128)S(1)}, u32[]{:S(2)}, u32[]{:S(2)}) async-start(f32[2,192,1280]{2,1,0:T(8,128)} %fusion.16), calls=%async_computation.6 | async-start | bytes 3932160 | tf_op jit(solution)/shard_map/all_to_all | solution.py:35
  143.4 47.1 %copy-start.7 = (f32[6,256,32]{1,2,0:T(8,128)S(1)}, f32[6,256,32]{1,2,0:T(8,128)}, u32[]{:S(2)}) copy-start(f32[6,256,32]{1,2,0:T(8,128)} %get-tuple-element.9) | copy-start | bytes 589828
  163.3 22.9 %all-to-all-start.5 = ((bf16[96,1,2,1280]{3,2,1,0:T(2,128)(2,1)}), bf16[96,1,2,1280]{3,2,1,0:T(2,128)(2,1)S(1)}, u32[]{:S(2)}, u32[]{:S(2)}) async-start(bf16[96,1,2,1280]{3,2,1,0:T(2,128)(2,1)} %reshape.82), calls=%async_computation.5 | async-start | bytes 983040 | tf_op jit(solution)/shard_map/all_to_all | solution.py:140
  186.2 19.4 %all-to-all-start.7 = ((bf16[96,1,2,1280]{3,2,1,0:T(2,128)(2,1)}), bf16[96,1,2,1280]{3,2,1,0:T(2,128)(2,1)S(1)}, u32[]{:S(2)}, u32[]{:S(2)}) async-start(bf16[96,1,2,1280]{3,2,1,0:T(2,128)(2,1)} %convert_element_type.73), calls=%async_computation.7 | async-start | bytes 983040 | tf_op jit(solution)/shard_map/all_to_all | solution.py:120
  189.7 283.2 %all-reduce.3.cloned.1.call-start = ((), (), s32[]{:S(2)}) async-start(), calls=%async_computation.10 | async-start | bytes 327680 | tf_op jit(solution)/shard_map/psum | solution.py:147
  206.2 3.7 copy-start.3
  209.9 263.1 %copy-start.6 = (bf16[384,1280]{1,0:T(8,128)(2,1)S(1)}, bf16[384,1280]{1,0:T(8,128)(2,1)}, u32[]{:S(2)}) copy-start(bf16[384,1280]{1,0:T(8,128)(2,1)} %reshape_reshape.7) | copy-start | bytes 2949124
  212.8 378.6 %all-reduce.5.cloned.1.call-start = ((), (), s32[]{:S(2)}) async-start(), calls=%async_computation.11 | async-start | bytes 327680 | tf_op jit(solution)/shard_map/psum | solution.py:147
  472.9 5.4 copy-start.5
  472.9 156.2 %reduce-scatter.3.cloned.1.call-start = ((), (), s32[]{:S(2)}) async-start(), calls=%async_computation.12 | async-start | bytes 3686400 | tf_op jit(solution)/shard_map/reduce_scatter | solution.py:149
  478.0 230.0 %reduce-scatter.5.cloned.1.call-start = ((), (), s32[]{:S(2)}) async-start(), calls=%async_computation.13 | async-start | bytes 3686400 | tf_op jit(solution)/shard_map/reduce_scatter | solution.py:154
  483.2 5.5 copy-start.9
  582.8 126.8 %copy-start.1 = (bf16[1,1280,1280]{2,1,0:T(8,128)(2,1)S(1)}, bf16[1,1280,1280]{2,1,0:T(8,128)(2,1)}, u32[]{:S(2)}) copy-start(bf16[1,1280,1280]{2,1,0:T(8,128)(2,1)} %param.10) | copy-start | bytes 9830404
Sparse Core Ops, SparseCore 0:
  212.9 259.9 all-reduce.2
  475.5 69.3 all-reduce.4
  548.1 81.0 reduce-scatter.2
  632.1 75.8 reduce-scatter.4
